TPU v7x, 32 devices: a whole 2x2x4 slice. The times are simulated.
32 devices in a mesh: dp: 8 (over z, x), mp: 4 (over y, core).
Axes of the slice: x: 2, y: 2, z: 4, core: 2. Of those that a mesh axis runs over, the one named last changes fastest.
Arguments:
- pool_inputs: bfloat16 [1024, 8, 4096], P('dp', None, 'mp'), may hold values from -6 to 6
- pool_targets: bfloat16 [1024, 8, 4096], P('dp', None, 'mp'), may hold values from -6 to 6
- frozen: bfloat16 [4096, 4096], P(None, 'mp'), may hold values from -0.09375 to 0.09375
- gain: float32 [4096], P('mp'), may hold values from 0.5 to 1.5
- adapter_down: bfloat16 [8, 64, 4096], P('dp', None, 'mp'), may hold values from -0.09375 to 0.09375
- adapter_up: bfloat16 [8, 64, 4096], P('dp', None, 'mp'), may hold values from -0.75 to 0.75
- sample_ids: int32 [512], P('dp'), may hold values from 0 to 127
- buckets: int32 [1024], P('dp'), may hold values from 0 to 15
- lengths: int32 [1024], P('dp'), may hold values from 1 to 8
- destinations: int32 [512, 1], P('dp'), may hold values from 0 to 7; in each aligned block of 64 rows (0 to 63, 64 to 127, ...) at most 12 rows name the same one
- competence: float32 [1], replicated, may hold values from 0.3 to 0.7
Outputs:
- grad_down: float32 [8, 64, 4096], P('dp', None, 'mp')
- grad_up: float32 [8, 64, 4096], P('dp', None, 'mp')
- bucket_loss: float32 [16], replicated
- competence_next: float32 [1], replicated
Inputs may be any that keep to these rules, and one draw needn't show every extreme that they name: `destinations`: of the 64 sampled slots of one holder, at most 12 name the same trainer. `sample_ids`: an index into the holder's own 128 stored blocks.
All inputs are finite; a program needn't handle non-finite values.
Results may differ from a plain program's by a relative error of at most 0.0056.
Values may be sent and summed in bfloat16 or wider, within the bound.
A program may use at most 128 MiB of HBM per device.

v0:
```python
import jax
import jax.numpy as jnp
from jax import lax
from jax.sharding import PartitionSpec as P

NB = 16


RMS_EPSILON = 1e-05
SHARPNESS = 12.0
ADAPTER_SCALING = 2.0


def normalize(values, gain, model_width):
    partial_value = jnp.sum(values * values, axis=1)
    square_total = lax.psum(partial_value, "mp")
    inverse_rms = lax.rsqrt(square_total / model_width + RMS_EPSILON)
    return (values * inverse_rms[:, None] * gain[None, :]).astype(jnp.bfloat16)


def frozen_gap(values, normed, targets, frozen):
    projected = jnp.dot(
        lax.all_gather(normed, "mp", axis=1, tiled=True), frozen, preferred_element_type=jnp.float32
    )
    return (values + projected - targets.astype(jnp.float32)).astype(jnp.bfloat16)


def place_blocks(placing, sequence_blocks):
    flat_blocks = sequence_blocks.reshape(sequence_blocks.shape[0], -1)
    return jnp.dot(placing, flat_blocks, preferred_element_type=jnp.float32).astype(jnp.bfloat16)


def on_device(
    pool_inputs,
    pool_targets,
    frozen,
    gain,
    adapter_down,
    adapter_up,
    sample_ids,
    buckets,
    lengths,
    destinations,
    competence,
):
    trainers = lax.axis_size("dp")
    sampled = sample_ids.shape[0]
    pool_rows, block_len, feature_part = pool_inputs.shape
    model_width = frozen.shape[0]
    per_pair = max(2, 3 * sampled // (2 * trainers))
    block_capacity = trainers * per_pair
    choosing = sample_ids[:, None] == jnp.arange(pool_rows, dtype=jnp.int32)[None, :]
    chosen_buckets = jnp.sum(jnp.where(choosing, buckets[None, :], 0), axis=1)
    chosen_lengths = jnp.sum(jnp.where(choosing, lengths[None, :], 0), axis=1)
    chosen_inputs = jnp.take(pool_inputs, sample_ids, axis=0)
    chosen_targets = jnp.take(pool_targets, sample_ids, axis=0)
    bucket_range = jnp.arange(NB, dtype=jnp.int32)
    all_buckets, all_lengths = (
        lax.all_gather(chosen_buckets, "dp", axis=0, tiled=True),
        lax.all_gather(chosen_lengths, "dp", axis=0, tiled=True),
    )
    table_onehot = (all_buckets[:, None] == bucket_range[None, :]).astype(jnp.float32)
    counts = jnp.sum(table_onehot * all_lengths[:, None].astype(jnp.float32), axis=0)
    floor_counts = jnp.maximum(counts, 1.0)
    weights = jax.nn.sigmoid(
        SHARPNESS * (competence[0] - (bucket_range.astype(jnp.float32) + 0.5) / NB)
    )
    target_trainer = destinations[:, 0]
    same_dest = target_trainer[:, None] == target_trainer[None, :]
    earlier = jnp.arange(sampled)[None, :] < jnp.arange(sampled)[:, None]
    arrival = jnp.sum((same_dest & earlier).astype(jnp.int32), axis=1)
    slot_index = target_trainer * per_pair + arrival
    slot_match = jnp.arange(block_capacity, dtype=jnp.int32)[:, None] == slot_index[None, :]
    placing = slot_match.astype(jnp.bfloat16)
    slot_bucket = jnp.sum(jnp.where(slot_match, chosen_buckets[None, :], 0), axis=1)
    slot_length = jnp.sum(jnp.where(slot_match, chosen_lengths[None, :], 0), axis=1)
    slot_info = jnp.stack([slot_bucket, slot_length], axis=1)
    send_inputs = place_blocks(placing, chosen_inputs)
    send_targets = place_blocks(placing, chosen_targets)
    got_inputs, got_targets, got_info = (
        lax.all_to_all(send_inputs, "dp", split_axis=0, concat_axis=0, tiled=True),
        lax.all_to_all(send_targets, "dp", split_axis=0, concat_axis=0, tiled=True),
        lax.all_to_all(slot_info, "dp", split_axis=0, concat_axis=0, tiled=True),
    )
    values = got_inputs.reshape(block_capacity * block_len, feature_part).astype(jnp.float32)
    normed = normalize(values, gain, model_width)
    base_gap = frozen_gap(
        values, normed, got_targets.reshape(block_capacity * block_len, feature_part), frozen
    )
    slot_onehot = (got_info[:, 0][:, None] == bucket_range[None, :]).astype(jnp.float32)
    live_mask = (
        (jnp.arange(block_len, dtype=jnp.int32)[None, :] < got_info[:, 1][:, None])
        .astype(jnp.float32)
        .reshape(-1)
    )
    block_coefficient = jnp.sum(slot_onehot * (weights / floor_counts)[None, :], axis=1)
    row_coefficient = jnp.repeat(block_coefficient, block_len)
    down_map = adapter_down[0]
    up_map = adapter_up[0]
    contract_last = (((1,), (1,)), ((), ()))
    contract_first = (((0,), (0,)), ((), ()))
    latent_part = lax.dot_general(
        normed, down_map, contract_last, preferred_element_type=jnp.float32
    )
    latent_rows = lax.psum(latent_part, "mp")
    lowered_rows = (ADAPTER_SCALING * latent_rows).astype(jnp.bfloat16)
    distance = base_gap.astype(jnp.float32) + jnp.dot(
        lowered_rows, up_map, preferred_element_type=jnp.float32
    )
    output_grad = ((2.0 * row_coefficient * live_mask)[:, None] * distance).astype(jnp.bfloat16)
    back_part = lax.dot_general(
        output_grad, up_map, contract_last, preferred_element_type=jnp.float32
    )
    latent_gradient = lax.psum(back_part, "mp")
    lowered_gradient = (ADAPTER_SCALING * latent_gradient).astype(jnp.bfloat16)
    up_gradient = lax.dot_general(
        lowered_rows, output_grad, contract_first, preferred_element_type=jnp.float32
    )
    down_gradient = lax.dot_general(
        lowered_gradient, normed, contract_first, preferred_element_type=jnp.float32
    )
    block_square = jnp.sum(
        (jnp.sum(distance * distance, axis=1) * live_mask).reshape(block_capacity, block_len),
        axis=1,
    )
    partial_value = jnp.sum(slot_onehot * block_square[:, None], axis=0)
    loss_sum = lax.psum(partial_value, ("dp", "mp"))
    bucket_loss = loss_sum / (floor_counts * model_width)
    progress = jnp.sum(weights * bucket_loss) / jnp.sum(bucket_loss)
    competence_next = competence + 0.5 * (1.0 - competence) * progress
    return (down_gradient[None], up_gradient[None], bucket_loss, competence_next)


def solution(mesh):
    in_specs = (
        P("dp", None, "mp"),
        P("dp", None, "mp"),
        P(None, "mp"),
        P("mp"),
        P("dp", None, "mp"),
        P("dp", None, "mp"),
        P("dp"),
        P("dp"),
        P("dp"),
        P("dp", None),
        P(),
    )
    out_specs = (P("dp", None, "mp"), P("dp", None, "mp"), P(), P())
    return jax.shard_map(
        on_device, mesh=mesh, in_specs=in_specs, out_specs=out_specs, check_vma=False
    )
```

profile of v0, /device:TPU:0, one launch (start us, length us, event | category | flops | bytes accessed | tf_op | source)
XLA Modules:
  0.0 246.0 jit_solution(13369916668289395877)
XLA Ops:
  7.2 0.0 copy-start
  7.2 0.0 all-gather.2.cloned.1.call-start
  7.2 0.8 compare_select_fusion
  8.0 0.7 compare_and_fusion
  8.7 0.1 copy-done
  8.8 0.6 gather_fusion.1
  9.4 3.2 %gather_fusion = bf16[64,8,1024]{2,1,0:T(8,128)(2,1)} fusion(bf16[128,8,1024]{2,1,0:T(8,128)(2,1)} %param.13, s32[1024]{0:T(1024)S(1)} %pad_clamp_fusion), kind=kCustom, calls=%fused_computation.clone | custom fusion | bytes 2097408 | tf_op jit(solution)/shard_map/jit(_take)/gather | solution.py:55
  12.6 2.5 %broadcast_select_fusion = (bf16[64,8,1024]{2,1,0:T(8,128)(2,1)}, bf16[64,8,1024]{2,1,0:T(8,128)(2,1)S(1)}) fusion(bf16[64,8,1024]{2,1,0:T(8,128)(2,1)S(1)} %gather_fusion.1, pred[64]{0:T(512)(128)(4,1)S(1)} %compare_and_fusion, bf16[64,8,1024]{2,1,0:T(8,128)(2,1)} %gather_fusion), kind=kLoop, calls=%fused_computation.15 | loop fusion | flops 1048576 | bytes 4194368 | tf_op jit(solution)/shard_map/jit(_take)/select_n | solution.py:56
  15.1 0.6 copy.28
  15.7 0.2 convert_reduce_fusion
  15.9 1.8 convolution_convert_fusion.1
  17.7 2.7 %all_to_all.20 = bf16[8,12,8192]{2,1,0:T(8,128)(2,1)} reshape(bf16[96,8192]{1,0:T(8,128)(2,1)} %convolution_convert_fusion.1) | data formatting | bytes 3145728 | tf_op jit(solution)/shard_map/all_to_all | solution.py:81
  20.4 55.6 %all_to_all.27 = bf16[8,12,8192]{2,1,0:T(8,128)(2,1)} all-to-all(bf16[8,12,8192]{2,1,0:T(8,128)(2,1)} %all_to_all.20), channel_id=1, replica_groups=mesh['dp'=8,'mp'=4] {'dp'}, dimensions={0} | all-to-all | bytes 3145728 | tf_op jit(solution)/shard_map/all_to_all | solution.py:81
  76.0 4.3 %reshape.121 = f32[768,1024]{1,0:T(8,128)} reshape(bf16[8,12,8192]{2,1,0:T(8,128)(2,1)} %all_to_all.27) | data formatting | bytes 4718592 | tf_op jit(solution)/shard_map/convert_element_type | solution.py:85
  80.2 2.2 multiply_reduce_fusion.1
  82.4 5.7 %psum.28 = f32[768]{0:T(1024)S(1)} all-reduce(f32[768]{0:T(1024)S(1)} %multiply_reduce_fusion.1), channel_id=1, replica_groups=mesh['dp'=8,'mp'=4] {'mp'}, use_global_device_ids=true, to_apply=%region_8.10 | all-reduce | flops 768 | bytes 6144 | tf_op jit(solution)/shard_map/psum | solution.py:16
  88.1 0.0 copy-start.8
  88.1 0.0 copy-start.9
  88.1 3.5 %multiply_convert_fusion.1 = bf16[768,1024]{1,0:T(8,128)(2,1)} fusion(f32[768,1024]{1,0:T(8,128)} %reshape.121, f32[1024]{0:T(1024)S(1)} %copy-done.6, f32[768]{0:T(1024)S(1)} %add_rsqrt_fusion), kind=kLoop, calls=%fused_computation.11 | loop fusion | flops 2359296 | bytes 4725760 | tf_op jit(solution)/shard_map/convert_element_type | solution.py:18
  91.6 0.0 all-gather.2.cloned.1.call-update
  91.7 0.2 select_reduce_fusion.5
  91.9 0.1 select_reduce_fusion.4
  92.0 0.1 stack.10
  92.1 0.1 stack.9
  92.2 0.6 copy.24
  92.8 4.2 %all-to-all-start = ((s32[8,12,2]{1,2,0:T(2,128)}), s32[8,12,2]{1,2,0:T(2,128)S(1)}, u32[]{:S(2)}, u32[]{:S(2)}) async-start(s32[8,12,2]{1,2,0:T(2,128)} %copy.24), calls=%async_computation | async-start | bytes 16384 | tf_op jit(solution)/shard_map/all_to_all | solution.py:83
  97.0 0.6 copy.29
  97.6 0.0 copy-start.11
  97.6 1.8 convolution_convert_fusion
  99.4 2.8 %all_to_all.22 = bf16[8,12,8192]{2,1,0:T(8,128)(2,1)} reshape(bf16[96,8192]{1,0:T(8,128)(2,1)} %convolution_convert_fusion) | data formatting | bytes 3145728 | tf_op jit(solution)/shard_map/all_to_all | solution.py:82
  102.2 0.6 dynamic-slice
  103.5 0.2 dynamic-update-slice.1
  103.7 0.2 dynamic-update-slice
  103.9 11.8 %all-reduce.2 = (s32[512]{0:T(512)S(1)}, s32[512]{0:T(512)S(1)}) all-reduce(s32[512]{0:T(512)S(1)} %dynamic-update-slice.1, s32[512]{0:T(512)S(1)} %dynamic-update-slice), channel_id=1, replica_groups=mesh['dp'=8,'mp'=4] {'dp'}, use_global_device_ids=true, to_apply=%add.1 | all-reduce | flops 1024 | bytes 8192
  115.8 4.4 %all-to-all-start.2 = ((bf16[8,12,8192]{2,1,0:T(8,128)(2,1)}), bf16[8,12,8192]{2,1,0:T(8,128)(2,1)}, u32[]{:S(2)}, u32[]{:S(2)}) async-start(bf16[8,12,8192]{2,1,0:T(8,128)(2,1)} %all_to_all.22), calls=%async_computation.2 | async-start | bytes 4194304 | tf_op jit(solution)/shard_map/all_to_all | solution.py:82
  120.1 0.0 all-reduce.6.cloned.1.call-start
  120.2 0.1 select_reduce_fusion.1
  121.0 0.1 all_to_all.19
  121.1 0.1 mul.157
  121.2 1.9 mul.158
  123.2 4.6 %mul.159 = f32[8,12,8192]{2,0,1:T(8,128)} reshape(f32[8,12,8,1024]{3,2,0,1:T(8,128)} %mul.158) | data formatting | bytes 6291456 | tf_op jit(solution)/shard_map/mul | solution.py:18
  127.7 5.8 %fusion.1 = bf16[8,12,8192]{2,1,0:T(8,128)(2,1)} fusion(f32[8,12,8192]{2,0,1:T(8,128)} %mul.159, f32[8192]{0:T(1024)S(1)} %bitcast.52, bf16[8,12,8192]{2,1,0:T(8,128)(2,1)} %all_to_all.27), kind=kLoop, calls=%fused_computation.6 | loop fusion | flops 3145728 | bytes 6324224 | tf_op jit(solution)/shard_map/convert_element_type | solution.py:18
  133.5 4.0 %convert_element_type.87 = bf16[768,1024]{1,0:T(8,128)(2,1)} reshape(bf16[8,12,8192]{2,1,0:T(8,128)(2,1)} %fusion.1) | data formatting | bytes 3145728 | tf_op jit(solution)/shard_map/convert_element_type | solution.py:18
  137.5 2.7 %fusion.6 = f32[768,64]{0,1:T(8,128)} fusion(bf16[768,1024]{1,0:T(8,128)(2,1)} %convert_element_type.87, bf16[1,64,1024]{2,1,0:T(8,128)(2,1)S(1)} %copy-done.5), kind=kOutput, calls=%fused_computation.23 | convolution fusion | flops 100663296 | bytes 1900544 | tf_op jit(solution)/shard_map/dot_general | solution.py:102
  140.2 0.0 all-reduce.6.cloned.1.call-update
  140.2 0.2 all-reduce.8.cloned.1.call-start
  140.5 25.2 %all-to-all-done.2 = bf16[8,12,8192]{2,1,0:T(8,128)(2,1)} async-done(((bf16[8,12,8192]{2,1,0:T(8,128)(2,1)}), bf16[8,12,8192]{2,1,0:T(8,128)(2,1)}, u32[]{:S(2)}, u32[]{:S(2)}) %all-to-all-start.2) | async-done | bytes 1572896 | tf_op jit(solution)/shard_map/all_to_all | solution.py:82
  165.7 4.2 %reshape.122 = f32[768,1024]{1,0:T(8,128)} reshape(bf16[8,12,8192]{2,1,0:T(8,128)(2,1)} %all-to-all-done.2) | data formatting | bytes 4718592 | tf_op jit(solution)/shard_map/convert_element_type | solution.py:25
  169.9 13.5 %subtract_convert_fusion = bf16[768,1024]{1,0:T(8,128)(2,1)} fusion(f32[768,1024]{1,0:T(8,128)} %reshape.122, f32[768,1024]{1,0:T(8,128)} %reshape.121, bf16[768,4096]{1,0:T(8,128)(2,1)} %all-gather.2.cloned.1.call-done, bf16[4096,1024]{1,0:T(8,128)(2,1)} %param.15), kind=kOutput, calls=%fused_computation.10 | convolution fusion | flops 6444810240 | bytes 22544384 | tf_op jit(solution)/shard_map/dot_general | solution.py:22
  183.4 3.8 %multiply_reduce_fusion = (f32[768]{0:T(1024)S(1)}, f32[768,1024]{1,0:T(8,128)}) fusion(bf16[768,1024]{1,0:T(8,128)(2,1)} %subtract_convert_fusion, bf16[1,64,1024]{2,1,0:T(8,128)(2,1)S(1)} %copy-done.4, f32[768,64]{0,1:T(8,128)} %all-reduce.6.cloned.1.call-done), kind=kOutput, calls=%fused_computation.7 | convolution fusion | flops 103906560 | bytes 5049344 | tf_op jit(solution)/shard_map/dot_general | solution.py:107
  187.2 0.1 reduce_sum.128
  187.3 0.2 select_reduce_fusion
  187.4 0.1 select_reduce_fusion.6
  187.6 0.1 fusion.9
  187.7 0.1 mul.150
  187.8 2.8 %multiply_convert_fusion = bf16[768,1024]{1,0:T(8,128)(2,1)S(1)} fusion(f32[768,1024]{1,0:T(8,128)} %get-tuple-element.21, bf16[768,1024]{1,0:T(8,128)(2,1)} %subtract_convert_fusion, f32[768]{0:T(1024)S(1)} %mul.150), kind=kLoop, calls=%fused_computation.8 | loop fusion | flops 3145728 | bytes 6294528 | tf_op jit(solution)/shard_map/convert_element_type | solution.py:110
  190.6 1.1 copy-done.1
  191.7 1.3 fusion.2
  193.0 0.0 all-reduce.8.cloned.1.call-update
  193.0 37.7 %psum.31 = f32[16]{0:T(128)S(1)} all-reduce(f32[16]{0:T(128)S(1)} %get-tuple-element.7), channel_id=1, replica_groups=mesh['dp'=8,'mp'=4] {'dp','mp'}, use_global_device_ids=true, to_apply=%region_14.16 | all-reduce | flops 16 | bytes 128 | tf_op jit(solution)/shard_map/psum | solution.py:127
  230.7 1.1 fusion.17
  231.9 2.5 %convolution_bitcast_fusion = f32[1,64,1024]{2,1,0:T(8,128)} fusion(bf16[768,1024]{1,0:T(8,128)(2,1)} %copy-done.1, f32[768,64]{0,1:T(8,128)S(1)} %copy-done.3), kind=kOutput, calls=%fused_computation.13 | convolution fusion | flops 100761600 | bytes 2031616 | tf_op jit(solution)/shard_map/dot_general | solution.py:116
  235.7 0.0 all-reduce.8.cloned.1.call-done
  235.7 2.6 %convolution_bitcast_fusion.1 = f32[1,64,1024]{2,1,0:T(8,128)} fusion(bf16[768,1024]{1,0:T(8,128)(2,1)} %multiply_convert_fusion.1, f32[768,64]{0,1:T(8,128)} %all-reduce.8.cloned.1.call-done), kind=kOutput, calls=%fused_computation.14 | convolution fusion | flops 100761600 | bytes 2031616 | tf_op jit(solution)/shard_map/dot_general | solution.py:119
  (35 shorter events, 0.1 us)
Async XLA Ops:
  7.2 1.6 copy-start
  7.2 162.7 %all-gather.2.cloned.1.call-start = ((), (), s32[]{:S(2)}) async-start(), calls=%async_computation.3 | async-start | bytes 7864320 | tf_op jit(solution)/shard_map/all_gather | solution.py:23
  12.6 3.1 %copy-start.10 = (s32[64,1]{0,1:T(1,128)S(1)}, s32[64,1]{0,1:T(1,128)}, u32[]{:S(2)}) copy-start(s32[64,1]{0,1:T(1,128)} %param.22) | copy-start | bytes 772
  76.0 12.1 %copy-start.6 = (f32[1024]{0:T(1024)S(1)}, f32[1024]{0:T(1024)}, u32[]{:S(2)}) copy-start(f32[1024]{0:T(1024)} %param.16) | copy-start | bytes 12292
  88.1 3.6 %copy-start.7 = (s32[64]{0:T(128)S(1)}, s32[64]{0:T(128)}, u32[]{:S(2)}) copy-start(s32[64]{0:T(128)} %param.19) | copy-start | bytes 772
  88.1 3.6 %copy-start.8 = (s32[128]{0:T(128)S(1)}, s32[128]{0:T(128)}, u32[]{:S(2)}) copy-start(s32[128]{0:T(128)} %param.20) | copy-start | bytes 1540
  88.1 3.6 %copy-start.9 = (s32[128]{0:T(128)S(1)}, s32[128]{0:T(128)}, u32[]{:S(2)}) copy-start(s32[128]{0:T(128)} %param.21) | copy-start | bytes 1540
  88.1 8.9 %copy-start.2 = (bf16[64,8,1024]{2,1,0:T(8,128)(2,1)S(1)}, bf16[64,8,1024]{2,1,0:T(8,128)(2,1)}, u32[]{:S(2)}) copy-start(bf16[64,8,1024]{2,1,0:T(8,128)(2,1)} %get-tuple-element.18) | copy-start | bytes 3145732
  92.8 23.0 %all-to-all-start = ((s32[8,12,2]{1,2,0:T(2,128)}), s32[8,12,2]{1,2,0:T(2,128)S(1)}, u32[]{:S(2)}, u32[]{:S(2)}) async-start(s32[8,12,2]{1,2,0:T(2,128)} %copy.24), calls=%async_computation | async-start | bytes 16384 | tf_op jit(solution)/shard_map/all_to_all | solution.py:83
  97.6 4.6 %copy-start.11 = (u32[32]{0:T(128)S(1)}, u32[32]{0:T(128)}, u32[]{:S(2)}) copy-start(u32[32]{0:T(128)} %constant.48) | copy-start | bytes 388
  115.8 49.9 %all-to-all-start.2 = ((bf16[8,12,8192]{2,1,0:T(8,128)(2,1)}), bf16[8,12,8192]{2,1,0:T(8,128)(2,1)}, u32[]{:S(2)}, u32[]{:S(2)}) async-start(bf16[8,12,8192]{2,1,0:T(8,128)(2,1)} %all_to_all.22), calls=%async_computation.2 | async-start | bytes 4194304 | tf_op jit(solution)/shard_map/all_to_all | solution.py:82
  120.1 63.2 %all-reduce.6.cloned.1.call-start = ((), (), s32[]{:S(2)}) async-start(), calls=%async_computation.4 | async-start | bytes 393216 | tf_op jit(solution)/shard_map/psum | solution.py:105
  133.5 4.0 %copy-start.5 = (bf16[1,64,1024]{2,1,0:T(8,128)(2,1)S(1)}, bf16[1,64,1024]{2,1,0:T(8,128)(2,1)}, u32[]{:S(2)}) copy-start(bf16[1,64,1024]{2,1,0:T(8,128)(2,1)} %param.17) | copy-start | bytes 393220
  140.2 95.5 %all-reduce.8.cloned.1.call-start = ((), (), s32[]{:S(2)}) async-start(), calls=%async_computation.5 | async-start | bytes 393216 | tf_op jit(solution)/shard_map/psum | solution.py:114
  169.9 13.5 %copy-start.4 = (bf16[1,64,1024]{2,1,0:T(8,128)(2,1)S(1)}, bf16[1,64,1024]{2,1,0:T(8,128)(2,1)}, u32[]{:S(2)}) copy-start(bf16[1,64,1024]{2,1,0:T(8,128)(2,1)} %param.18) | copy-start | bytes 393220
  187.7 44.1 %copy-start.3 = (f32[768,64]{0,1:T(8,128)S(1)}, f32[768,64]{0,1:T(8,128)}, u32[]{:S(2)}) copy-start(f32[768,64]{0,1:T(8,128)} %all-reduce.6.cloned.1.call-done) | copy-start | bytes 589828
  190.5 1.2 copy-start.1
Sparse Core Ops, SparseCore 0:
  91.8 45.5 all-gather.1
  140.4 32.9 all-reduce.5
  193.1 31.0 all-reduce.7
where the time goes:
time: 248 us; the launch traced here: 246 us
  blocking collectives  111 us (45%)
  local copies, waits for them, and re-layouts  32.8 us (13%)
  matrix products  30 us (12%)
  waiting for transfers between devices  25.3 us (10%)
  other arithmetic  20.3 us (8%)
  between operations  17.8 us (7%)
  starting transfers between devices  8.85 us (4%)
    all_to_all x1, blocking collectives, on_device(): lax.all_to_all(send_inputs, 'dp', split_axis=0, concat_axis=0, tiled=True)  55.6 us
    psum x1, blocking collectives, on_device(): loss_sum = lax.psum(partial_value, ('dp', 'mp'))  37.7 us
    all_to_all x1, waiting for transfers between devices, on_device(): lax.all_to_all(send_targets, 'dp', split_axis=0, concat_axis=0, tiled=True)  25.2 us
    dot_general x1, matrix products, frozen_gap(): jnp.dot(lax.all_gather(normed, 'mp', axis=1, tiled=True), frozen, preferr...  13.5 us
    unnamed x1, blocking collectives  11.8 us
    convert_element_type x2, other arithmetic, normalize(): return (values * inverse_rms[:, None] * gain[None, :]).astype(jnp.bfloat16)  9.29 us
    mul x4, local copies, waits for them, and re-layouts, normalize(): return (values * inverse_rms[:, None] * gain[None, :]).astype(jnp.bfloat16)  6.63 us
    psum x1, blocking collectives, normalize(): square_total = lax.psum(partial_value, 'mp')  5.67 us
  transfers between devices with their start and end apart: 5, of which 1 were waited for; matrix products, arithmetic and copies ran while one was open for 18% of the time, Pallas kernels for 0%

commit v1 on v0

--- a/solution.py
+++ b/solution.py
@@ -1,6 +1,10 @@
+import functools
+
 import jax
 import jax.numpy as jnp
 from jax import lax
+from jax.experimental import pallas as pl
+from jax.experimental.pallas import tpu as pltpu
 from jax.sharding import PartitionSpec as P
 
 NB = 16
@@ -131,7 +135,481 @@
     return (down_gradient[None], up_gradient[None], bucket_loss, competence_next)
 
 
+CONTRACT_LAST = (((1,), (1,)), ((), ()))
+CONTRACT_FIRST = (((0,), (0,)), ((), ()))
+LANES = 128
+CHUNKS = 4
+
+
+def fused_kernel(
+    ids_ref, dest_ref, bucket_ref, length_ref, comp_ref, gain_ref, x_ref, t_ref, frozen_ref, down_ref, up_ref,
+    gd_ref, gu_ref, loss_ref, next_ref,
+    frozen_buf, x_full, n_full, gain_full, adapters, counts_buf, loss_mp, loss_dp,
+    m_dest, m_coef, m_live, m_bucket, gap, spread, grad_out, lat_own, lat_pair, lat_send, lat_recv,
+    grads, x_out, x_in, z_out, z_up, z_down,
+    local_sem, xs_sem, xr_sem, gain_s, gain_r, au_s, au_r, ad_s, ad_r, ax_s, ax_r, cnt_s, cnt_r,
+    lm_s, lm_r, ld_s, ld_r, l1_s, l1_r, l2_s, l2_r, gx_s, gx_r, gu_s, gu_r, gdn_s, gdn_r,
+):
+    n_dp, n_mp = lax.axis_size("dp"), lax.axis_size("mp")
+    d, m = lax.axis_index("dp"), lax.axis_index("mp")
+    levels = n_dp // 2
+    z, xx = d // 2, d % 2
+    tokens, part = x_ref.shape
+    rank = down_ref.shape[1]
+    blocks = ids_ref.shape[0]
+    block_len = tokens // blocks
+    groups = n_dp * rank // LANES
+    per_group = LANES // rank
+    width = n_mp * part
+    chunk = tokens // CHUNKS
+    half = tokens // 2
+    y, core = m // 2, m % 2
+    partner, across = y * 2 + (1 - core), (1 - y) * 2 + core
+    diagonal = (1 - y) * 2 + (1 - core)
+    x_peer = z * 2 + (1 - xx)
+    f32, bf16 = jnp.float32, jnp.bfloat16
+    pending = []
+
+    def remote(src, dst, s_sem, r_sem, to):
+        return pltpu.make_async_remote_copy(
+            src_ref=src, dst_ref=dst, send_sem=s_sem, recv_sem=r_sem,
+            device_id=to, device_id_type=pl.DeviceIdType.MESH,
+        )
+
+    def send(make, when=None):
+        if when is None:
+            make().start()
+        else:
+            pl.when(when)(lambda: make().start())
+        pending.append((make, when))
+
+    barrier = pltpu.get_barrier_semaphore()
+    for j in range(1, n_dp):
+        pl.semaphore_signal(barrier, inc=1, device_id=((d + j) % n_dp, m), device_id_type=pl.DeviceIdType.MESH)
+    for j in range(1, n_mp):
+        pl.semaphore_signal(barrier, inc=1, device_id=(d, (m + j) % n_mp), device_id_type=pl.DeviceIdType.MESH)
+    own_down = pltpu.make_async_copy(down_ref.at[0], adapters.at[0, d], local_sem.at[0])
+    own_up = pltpu.make_async_copy(up_ref.at[0], adapters.at[1, d], local_sem.at[1])
+    own_x = pltpu.make_async_copy(x_ref, x_full.at[m], local_sem.at[2])
+    own_frozen = pltpu.make_async_copy(frozen_ref, frozen_buf, local_sem.at[3])
+    own_down.start()
+    own_up.start()
+    own_x.start()
+    pl.semaphore_wait(barrier, n_dp - 1 + n_mp - 1)
+
+    def x_copy(kind, i):
+        rows = pl.ds(i * chunk, chunk)
+        if kind == 0:
+            return remote(x_ref.at[rows], x_full.at[m, rows], xs_sem.at[0, i], xr_sem.at[0, i], (d, across))
+        if kind == 1:
+            return remote(x_ref.at[rows], x_full.at[m, rows], xs_sem.at[1, i], xr_sem.at[1, i], (d, partner))
+        return remote(
+            x_full.at[across, rows], x_full.at[across, rows], xs_sem.at[2, i], xr_sem.at[2, i], (d, partner)
+        )
+
+    def x_wait(kind, i):
+        rows = pl.ds(i * chunk, chunk)
+        slot = (across, partner, diagonal)[kind]
+        view = x_full.at[slot, rows]
+        remote(view, view, xs_sem.at[kind, i], xr_sem.at[kind, i], (d, partner)).wait_recv()
+
+    for i in range(CHUNKS):
+        send(functools.partial(x_copy, 0, i))
+    own_down.wait()
+    own_up.wait()
+
+    def a_copy(kind, zt, to):
+        s_sem, r_sem = ((au_s, au_r), (ad_s, ad_r), (ax_s, ax_r))[kind]
+        view = adapters.at[:, zt * 2 + xx]
+        return remote(view, view, s_sem.at[zt], r_sem.at[zt], (to, m))
+
+    def a_wait(kind, zt, slot):
+        s_sem, r_sem = ((au_s, au_r), (ad_s, ad_r), (ax_s, ax_r))[kind]
+        view = adapters.at[:, slot]
+        remote(view, view, s_sem.at[zt], r_sem.at[zt], (x_peer, m)).wait_recv()
+
+    send(lambda: a_copy(2, z, x_peer))
+    send(lambda: a_copy(0, z, d + 2), z < levels - 1)
+    send(lambda: a_copy(1, z, d - 2), z > 0)
+    for i in range(CHUNKS):
+        send(functools.partial(x_copy, 1, i))
+    gain_full[m] = gain_ref[...]
+    for j in range(1, n_mp):
+        send(
+            lambda j=j: remote(
+                gain_ref, gain_full.at[m], gain_s.at[j], gain_r.at[j], (d, (m + j) % n_mp)
+            )
+        )
+    own_frozen.start()
+
+    lane = lax.broadcasted_iota(jnp.int32, (tokens, LANES), 1)
+    row = lax.broadcasted_iota(jnp.int32, (tokens, LANES), 0)
+    lane64 = lax.broadcasted_iota(jnp.int32, (blocks, LANES), 1)
+    named = jnp.where(lane64 < LANES // 2, ids_ref[...], dest_ref[...]).astype(f32).astype(bf16)
+    spread_rows = (
+        lax.broadcasted_iota(jnp.int32, (tokens, blocks), 0) // block_len
+        == lax.broadcasted_iota(jnp.int32, (tokens, blocks), 1)
+    ).astype(f32).astype(bf16)
+    per_token = jnp.dot(spread_rows, named, preferred_element_type=f32)
+    token_id, token_dest = per_token[:, 0:1], per_token[:, LANES // 2:LANES // 2 + 1]
+    chosen = token_id == lane.astype(f32)
+    token_bucket = jnp.sum(jnp.where(chosen, bucket_ref[...].astype(f32), 0.0), axis=1, keepdims=True)
+    token_length = jnp.sum(jnp.where(chosen, length_ref[...].astype(f32), 0.0), axis=1, keepdims=True)
+    live = ((row % block_len).astype(f32) < token_length).astype(f32)
+    bucket_hot = (token_bucket == lane.astype(f32)).astype(f32)
+    m_dest[...] = jnp.broadcast_to(token_dest, (tokens, LANES))
+    m_live[...] = live
+    m_bucket[...] = bucket_hot
+    counts_buf[d] = jnp.broadcast_to(jnp.sum(bucket_hot * live, axis=0, keepdims=True), (8, LANES))
+
+    def spread_tile(buf, s_sem, r_sem, axis):
+        count, me = (n_dp, d) if axis == "dp" else (n_mp, m)
+        for j in range(1, count):
+            to = (me + j) % count
+            target = (to, m) if axis == "dp" else (d, to)
+            send(lambda j=j, target=target: remote(buf.at[me], buf.at[me], s_sem.at[j], r_sem.at[j], target))
+
+    def gather_tile(buf, s_sem, r_sem, axis):
+        count, me = (n_dp, d) if axis == "dp" else (n_mp, m)
+        for j in range(1, count):
+            source = (me + count - j) % count
+            target = (source, m) if axis == "dp" else (d, source)
+            remote(buf.at[source], buf.at[source], s_sem.at[j], r_sem.at[j], target).wait_recv()
+
+    own_x.wait()
+    for j in range(1, n_mp):
+        source = (m + n_mp - j) % n_mp
+        remote(gain_ref, gain_full.at[source], gain_s.at[j], gain_r.at[j], (d, source)).wait_recv()
+    spread_tile(counts_buf, cnt_s, cnt_r, "dp")
+
+    def normalise(i):
+        step = 32
+
+        def body(g, carry):
+            rows = pl.ds(pl.multiple_of(i * chunk + g * step, step), step)
+            total = jnp.zeros((step, 1), f32)
+            for k in range(n_mp):
+                v = x_full[k, rows, :].astype(f32)
+                total = total + jnp.sum(v * v, axis=1, keepdims=True)
+            inverse = lax.rsqrt(total / width + RMS_EPSILON)
+            for k in range(n_mp):
+                v = x_full[k, rows, :].astype(f32)
+                n_full[k, rows, :] = (v * inverse * gain_full[k]).astype(bf16)
+            return carry
+
+        lax.fori_loop(0, chunk // step, body, 0)
+
+    def project(h):
+        rows = pl.ds(h * half, half)
+        tile = 256
+
+        def body(n, carry):
+            cols = pl.ds(pl.multiple_of(n * tile, tile), tile)
+            acc = jnp.zeros((half, tile), f32)
+            for k in range(n_mp):
+                acc = acc + jnp.dot(
+                    n_full[k, rows, :], frozen_buf[pl.ds(k * part, part), cols], preferred_element_type=f32
+                )
+            gap[rows, cols] = (
+                x_ref[rows, cols].astype(f32) + acc - t_ref[rows, cols].astype(f32)
+            ).astype(bf16)
+            return carry
+
+        lax.fori_loop(0, part // tile, body, 0)
+
+    def relay(s):
+        @pl.when(z - s >= 0)
+        def _():
+            a_wait(0, z - s, (z - s) * 2 + xx)
+        send(lambda: a_copy(2, z - s, x_peer), z - s >= 0)
+        send(lambda: a_copy(0, z - s, d + 2), (z - s >= 0) & (z < levels - 1))
+
+        @pl.when(z + s < levels)
+        def _():
+            a_wait(1, z + s, (z + s) * 2 + xx)
+        send(lambda: a_copy(2, z + s, x_peer), z + s < levels)
+        send(lambda: a_copy(1, z + s, d - 2), (z + s < levels) & (z > 0))
+
+    for i in range(CHUNKS):
+        x_wait(0, i)
+        send(functools.partial(x_copy, 2, i))
+        if 1 <= i < levels:
+            relay(i)
+        x_wait(1, i)
+        x_wait(2, i)
+        normalise(i)
+        if i == CHUNKS // 2 - 1:
+            own_frozen.wait()
+            project(0)
+    for s in range(CHUNKS, levels):
+        relay(s)
+    for zt in range(levels):
+        a_wait(2, zt, zt * 2 + (1 - xx))
+
+    tile_rows = 128
+
+    def mask_of(rows, g):
+        who = lax.broadcasted_iota(jnp.int32, (tile_rows, LANES), 1) // rank + g * per_group
+        return who.astype(f32) == m_dest[rows, :]
+
+    def select(full, rows):
+        out = jnp.zeros((tile_rows, LANES), f32)
+        for g in range(groups):
+            out = out + jnp.where(mask_of(rows, g), full[:, g * LANES:(g + 1) * LANES], 0.0)
+        return out
+
+    def over_tiles(body):
+        def run(i, carry):
+            body(pl.ds(pl.multiple_of(i * tile_rows, tile_rows), tile_rows))
+            return carry
+
+        lax.fori_loop(0, tokens // tile_rows, run, 0)
+
+    def stack(which):
+        return adapters[which].reshape(n_dp * rank, part)
+
+    def first_half_sum(which):
+        send(
+            lambda: remote(
+                lat_own.at[which], lat_pair.at[which], l1_s.at[which], l1_r.at[which], (d, partner)
+            )
+        )
+
+    def second_half_sum(which):
+        remote(
+            lat_own.at[which], lat_pair.at[which], l1_s.at[which], l1_r.at[which], (d, partner)
+        ).wait_recv()
+        lat_send[which] = (lat_own[which] + lat_pair[which]).astype(bf16)
+        send(
+            lambda: remote(
+                lat_send.at[which], lat_recv.at[which], l2_s.at[which], l2_r.at[which], (d, across)
+            )
+        )
+
+    def finish_sum(which):
+        remote(
+            lat_send.at[which], lat_recv.at[which], l2_s.at[which], l2_r.at[which], (d, across)
+        ).wait_recv()
+
+        def body(rows):
+            total = lat_own[which, rows, :] + lat_pair[which, rows, :] + lat_recv[which, rows, :].astype(f32)
+            low = ADAPTER_SCALING * total
+            for g in range(groups):
+                spread[which, rows, g * LANES:(g + 1) * LANES] = jnp.where(mask_of(rows, g), low, 0.0).astype(bf16)
+
+        over_tiles(body)
+
+    def latent_body(rows):
+        full = lax.dot_general(n_full[m, rows, :], stack(0), CONTRACT_LAST, preferred_element_type=f32)
+        lat_own[0, rows, :] = select(full, rows)
+
+    over_tiles(latent_body)
+    first_half_sum(0)
+    gather_tile(counts_buf, cnt_s, cnt_r, "dp")
+    counts = counts_buf[0]
+    for k in range(1, n_dp):
+        counts = counts + counts_buf[k]
+    floor_counts = jnp.maximum(counts, 1.0)
+    bucket_lane = lax.broadcasted_iota(jnp.int32, (8, LANES), 1)
+    competence = comp_ref[...]
+    weights = jax.nn.sigmoid(SHARPNESS * (competence - (bucket_lane.astype(f32) + 0.5) / NB))
+    rate = jnp.where(bucket_lane < NB, weights / floor_counts, 0.0)[0:1]
+    coef = jnp.sum(m_bucket[...] * rate, axis=1, keepdims=True)
+    m_coef[...] = 2.0 * coef * m_live[...]
+    second_half_sum(0)
+    project(1)
+    finish_sum(0)
+
+    loss_mp[m] = jnp.zeros((8, LANES), f32)
+
+    def distance_body(rows):
+        delta = jnp.dot(spread[0, rows, :], stack(1), preferred_element_type=f32)
+        distance = gap[rows, :].astype(f32) + delta
+        square = jnp.sum(distance * distance, axis=1, keepdims=True)
+        loss_mp[m] += jnp.broadcast_to(
+            jnp.sum(m_bucket[rows, :] * (square * m_live[rows, :]), axis=0, keepdims=True), (8, LANES)
+        )
+        og = (m_coef[rows, 0:1] * distance).astype(bf16)
+        grad_out[rows, :] = og
+        back = lax.dot_general(og, stack(1), CONTRACT_LAST, preferred_element_type=f32)
+        lat_own[1, rows, :] = select(back, rows)
+
+    over_tiles(distance_body)
+    first_half_sum(1)
+
+    def gradient(h, values):
+        tile = 256
+
+        def body(n, carry):
+            cols = pl.ds(pl.multiple_of(n * tile, tile), tile)
+            out = lax.dot_general(spread[1 - h, :, :], values(cols), CONTRACT_FIRST, preferred_element_type=f32)
+            grads[h, :, :, cols] = out.reshape(n_dp, rank, tile)
+            return carry
+
+        lax.fori_loop(0, part // tile, body, 0)
+        for p in range(levels):
+            if p == levels - 1:
+                zt = z
+            else:
+                falling = levels - 1 - p
+                falling = jnp.where(falling > z, falling, falling - 1)
+                rising = jnp.where(p < z, p, p + 1)
+                zt = jnp.where(z < levels // 2, falling, rising)
+            x_out[h, zt] = grads[h, zt * 2 + (1 - xx)].astype(bf16)
+            send(
+                lambda zt=zt: remote(
+                    x_out.at[h, zt], x_in.at[h, zt], gx_s.at[h, zt], gx_r.at[h, zt], (x_peer, m)
+                )
+            )
+
+    gradient(1, lambda cols: grad_out[:, cols])
+    second_half_sum(1)
+    spread_tile(loss_mp, lm_s, lm_r, "mp")
+    finish_sum(1)
+    gradient(0, lambda cols: n_full[m, :, cols])
+
+    gather_tile(loss_mp, lm_s, lm_r, "mp")
+    total = loss_mp[0]
+    for k in range(1, n_mp):
+        total = total + loss_mp[k]
+    loss_dp[d] = total
+
+    def arrived(buf, h, zt, s_sem, r_sem):
+        view = buf.at[h, zt]
+        remote(view, view, s_sem.at[h, zt], r_sem.at[h, zt], (x_peer, m)).wait_recv()
+        grads[h, zt * 2 + xx] += buf[h, zt].astype(f32)
+
+    def pass_on(h, s):
+        def upward():
+            zt = z + s
+            arrived(x_in, h, zt, gx_s, gx_r)
+            pl.when(z > 0)(lambda: arrived(z_up, h, zt, gu_s, gu_r))
+            z_out[h, zt] = grads[h, zt * 2 + xx].astype(bf16)
+
+        def downward():
+            zt = z - s
+            arrived(x_in, h, zt, gx_s, gx_r)
+            pl.when(z < levels - 1)(lambda: arrived(z_down, h, zt, gdn_s, gdn_r))
+            z_out[h, zt] = grads[h, zt * 2 + xx].astype(bf16)
+
+        pl.when(z + s < levels)(upward)
+        send(
+            lambda: remote(
+                z_out.at[h, z + s], z_up.at[h, z + s], gu_s.at[h, z + s], gu_r.at[h, z + s], (d + 2, m)
+            ),
+            z + s < levels,
+        )
+        pl.when(z - s >= 0)(downward)
+        send(
+            lambda: remote(
+                z_out.at[h, z - s], z_down.at[h, z - s], gdn_s.at[h, z - s], gdn_r.at[h, z - s], (d - 2, m)
+            ),
+            z - s >= 0,
+        )
+
+    spread_tile(loss_dp, ld_s, ld_r, "dp")
+    for h, out_ref in ((1, gu_ref), (0, gd_ref)):
+        for s in range(levels - 1, 0, -1):
+            pass_on(h, s)
+        arrived(x_in, h, z, gx_s, gx_r)
+        pl.when(z > 0)(lambda h=h: arrived(z_up, h, z, gu_s, gu_r))
+        pl.when(z < levels - 1)(lambda h=h: arrived(z_down, h, z, gdn_s, gdn_r))
+        out_ref[0] = grads[h, d]
+
+    gather_tile(loss_dp, ld_s, ld_r, "dp")
+    loss_sum = loss_dp[0]
+    for k in range(1, n_dp):
+        loss_sum = loss_sum + loss_dp[k]
+    bucket_loss = jnp.where(bucket_lane < NB, loss_sum / (floor_counts * width), 0.0)
+    progress = jnp.sum(weights * bucket_loss, axis=1, keepdims=True) / jnp.sum(bucket_loss, axis=1, keepdims=True)
+    loss_ref[...] = bucket_loss[0:1]
+    next_ref[...] = (competence + 0.5 * (1.0 - competence) * jnp.broadcast_to(progress, (8, LANES)))[0:1]
+
+    for make, when in pending:
+        if when is None:
+            make().wait_send()
+        else:
+            pl.when(when)(lambda make=make: make().wait_send())
+
+
+def on_device_fused(
+    pool_inputs, pool_targets, frozen, gain, adapter_down, adapter_up, sample_ids, buckets, lengths, destinations,
+    competence,
+):
+    n_dp, n_mp = lax.axis_size("dp"), lax.axis_size("mp")
+    blocks = sample_ids.shape[0]
+    pool, block_len, part = pool_inputs.shape
+    rank = adapter_down.shape[1]
+    tokens = blocks * block_len
+    levels = n_dp // 2
+    x = pool_inputs.at[sample_ids].get(mode="promise_in_bounds").reshape(tokens, part)
+    t = pool_targets.at[sample_ids].get(mode="promise_in_bounds").reshape(tokens, part)
+    f32, bf16 = jnp.float32, jnp.bfloat16
+    vmem = pl.BlockSpec(memory_space=pltpu.VMEM)
+    dma = pltpu.SemaphoreType.DMA
+    out = pl.pallas_call(
+        fused_kernel,
+        out_shape=(
+            jax.ShapeDtypeStruct((1, rank, part), f32),
+            jax.ShapeDtypeStruct((1, rank, part), f32),
+            jax.ShapeDtypeStruct((1, LANES), f32),
+            jax.ShapeDtypeStruct((1, LANES), f32),
+        ),
+        in_specs=[vmem] * 8 + [pl.BlockSpec(memory_space=pl.ANY)] + [vmem] * 2,
+        out_specs=(vmem,) * 4,
+        scratch_shapes=[
+            pltpu.VMEM(frozen.shape, bf16),
+            pltpu.VMEM((n_mp, tokens, part), bf16),
+            pltpu.VMEM((n_mp, tokens, part), bf16),
+            pltpu.VMEM((n_mp, 1, part), f32),
+            pltpu.VMEM((2, n_dp, rank, part), bf16),
+            pltpu.VMEM((n_dp, 8, LANES), f32),
+            pltpu.VMEM((n_mp, 8, LANES), f32),
+            pltpu.VMEM((n_dp, 8, LANES), f32),
+            pltpu.VMEM((tokens, LANES), f32),
+            pltpu.VMEM((tokens, LANES), f32),
+            pltpu.VMEM((tokens, LANES), f32),
+            pltpu.VMEM((tokens, LANES), f32),
+            pltpu.VMEM((tokens, part), bf16),
+            pltpu.VMEM((2, tokens, n_dp * rank), bf16),
+            pltpu.VMEM((tokens, part), bf16),
+            pltpu.VMEM((2, tokens, LANES), f32),
+            pltpu.VMEM((2, tokens, LANES), f32),
+            pltpu.VMEM((2, tokens, LANES), bf16),
+            pltpu.VMEM((2, tokens, LANES), bf16),
+            pltpu.VMEM((2, n_dp, rank, part), f32),
+            pltpu.VMEM((2, levels, rank, part), bf16),
+            pltpu.VMEM((2, levels, rank, part), bf16),
+            pltpu.VMEM((2, levels, rank, part), bf16),
+            pltpu.VMEM((2, levels, rank, part), bf16),
+            pltpu.VMEM((2, levels, rank, part), bf16),
+            dma((4,)), dma((3, CHUNKS)), dma((3, CHUNKS)), dma((n_mp,)), dma((n_mp,)),
+            dma((levels,)), dma((levels,)), dma((levels,)), dma((levels,)), dma((levels,)), dma((levels,)),
+            dma((n_dp,)), dma((n_dp,)), dma((n_mp,)), dma((n_mp,)), dma((n_dp,)), dma((n_dp,)),
+            dma((2,)), dma((2,)), dma((2,)), dma((2,)),
+            dma((2, levels)), dma((2, levels)), dma((2, levels)), dma((2, levels)), dma((2, levels)), dma((2, levels)),
+        ],
+        compiler_params=pltpu.CompilerParams(
+            collective_id=0, has_side_effects=True, vmem_limit_bytes=58 * 2**20
+        ),
+        name="fused_step",
+    )(
+        sample_ids[:, None], destinations, buckets[None, :], lengths[None, :], competence[:, None], gain[None, :],
+        x, t, frozen, adapter_down, adapter_up,
+    )
+    return out[0], out[1], out[2][0, :NB], out[3][0, :1]
+
+
 def solution(mesh):
+    def pick(*args):
+        pool_inputs, frozen, adapter_down, sample_ids = args[0], args[2], args[4], args[6]
+        tokens, part = sample_ids.shape[0] * pool_inputs.shape[1], pool_inputs.shape[2]
+        n_dp, n_mp, rank = lax.axis_size("dp"), lax.axis_size("mp"), adapter_down.shape[1]
+        held = 2 * frozen.size + 4 * n_mp * tokens * part + (26 * n_dp + 16) * rank * part
+        fits = held < 44 * 2**20 and n_mp == 4 and n_dp % 2 == 0 and n_dp > 2
+        exact = pool_inputs.shape[0] == LANES and n_dp * rank % LANES == 0 and LANES % rank == 0
+        return (on_device_fused if fits and exact else on_device)(*args)
+
     in_specs = (
         P("dp", None, "mp"),
         P("dp", None, "mp"),
@@ -147,5 +625,5 @@
     )
     out_specs = (P("dp", None, "mp"), P("dp", None, "mp"), P(), P())
     return jax.shard_map(
-        on_device, mesh=mesh, in_specs=in_specs, out_specs=out_specs, check_vma=False
-    )
+        pick, mesh=mesh, in_specs=in_specs, out_specs=out_specs, check_vma=False
+    )

time: 248 us -> 120 us (0.48)
  blocking collectives: 111 us -> 0 us
  Pallas kernels: 0 us -> 104 us
  matrix products: 30 us -> 0 us
  waiting for transfers between devices: 25.3 us -> 0 us
  local copies, waits for them, and re-layouts: 32.8 us -> 12 us
  other arithmetic: 20.3 us -> 0.67 us
  between operations: 17.8 us -> 3.25 us
  starting transfers between devices: 8.85 us -> 0 us
    pallas_call x0 -> x1, Pallas kernels: none -> 104 us  [on_device_fused(): pl.pallas_call(fused_kernel, out_shape=(jax.ShapeDtypeStruct((1, rank, pa...]
    all_to_all x1 -> x0, blocking collectives: 55.6 us -> none  [on_device(): lax.all_to_all(send_inputs, 'dp', split_axis=0, concat_axis=0, tiled=True)]
    psum x2 -> x0, blocking collectives: 43.4 us -> none  [the longest x1 37.7 us: on_device(): loss_sum = lax.psum(partial_value, ('dp', 'mp'))]
    dot_general x8 -> x0, matrix products: 30 us -> none  [the longest x1 13.5 us: frozen_gap(): jnp.dot(lax.all_gather(normed, 'mp', axis=1, tiled=True), frozen, preferr...]
    all_to_all x2 -> x0, waiting for transfers between devices: 25.3 us -> none  [the longest x1 25.2 us: on_device(): lax.all_to_all(send_targets, 'dp', split_axis=0, concat_axis=0, tiled=True)]
    convert_element_type x3 -> x0, local copies, waits for them, and re-layouts: 12.4 us -> none  [the longest x1 4.25 us: on_device(): got_inputs.reshape(block_capacity * block_len, feature_part)]
    convert_element_type x4 -> x0, other arithmetic: 12.1 us -> none  [the longest x2 9.29 us: normalize(): return (values * inverse_rms[:, None] * gain[None, :]).astype(jnp.bfloat16)]
    unnamed x1 -> x0, blocking collectives: 11.8 us -> none
  transfers between devices with their start and end apart: 5 -> 0, of which waited for: 1 -> 0; matrix products, arithmetic and copies ran while one was open for 18% -> 0% of each run, Pallas kernels for 0% -> 0%
where the time goes in v1:
time: 120 us; the launch traced here: 119 us
  Pallas kernels  104 us (87%)
  local copies, waits for them, and re-layouts  12 us (10%)
  between operations  3.25 us (3%)
    pallas_call x1, Pallas kernels, on_device_fused(): pl.pallas_call(fused_kernel, out_shape=(jax.ShapeDtypeStruct((1, rank, pa...  104 us
    unnamed x5, local copies, waits for them, and re-layouts  4.71 us
    gather x1, local copies, waits for them, and re-layouts, on_device_fused(): pool_inputs.at[sample_ids].get(mode='promise_in_bounds')  3.18 us

profile of v1, /device:TPU:0, one launch (start us, length us, event | category | flops | bytes accessed | tf_op | source)
XLA Modules:
  0.0 119.4 jit_solution(6955915370275713860)
XLA Ops:
  0.6 0.0 copy-start
  1.4 0.7 compare_select_fusion
  2.1 1.4 %copy.16.dest_ref = s32[64,1]{1,0:T(8,128)} copy(s32[64,1]{0,1:T(1,128)} %param.20) | data formatting | bytes 512 | tf_op args[9]
  3.5 1.4 %copy.15.ids_ref = s32[64,1]{1,0:T(8,128)} copy(s32[64,1]{0,1:T(1,128)} %bitcast.15) | data formatting | bytes 512 | tf_op jit(solution)/shard_map/broadcast_in_dim | solution.py:597
  4.8 0.0 copy-done
  4.8 1.6 %gather_fusion.1 = bf16[64,8,1024]{2,1,0:T(8,128)(2,1)} fusion(bf16[128,8,1024]{2,1,0:T(8,128)(2,1)S(1)} %copy-done, s32[1024]{0:T(1024)S(1)} %pad_clamp_fusion), kind=kCustom, calls=%fused_computation.1 | custom fusion | bytes 2097408 | tf_op jit(solution)/shard_map/gather | solution.py:546
  6.5 3.2 %gather_fusion = bf16[64,8,1024]{2,1,0:T(8,128)(2,1)} fusion(bf16[128,8,1024]{2,1,0:T(8,128)(2,1)} %param.11, s32[1024]{0:T(1024)S(1)} %pad_clamp_fusion), kind=kCustom, calls=%fused_computation | custom fusion | bytes 2097408 | tf_op jit(solution)/shard_map/gather | solution.py:545
  9.6 103.5 %fused_step.1 = (f32[1,64,1024]{2,1,0:T(8,128)}, f32[1,64,1024]{2,1,0:T(8,128)}, f32[1,128]{1,0:T(1,128)}, f32[1,128]{1,0:T(1,128)}) custom-call(s32[64,1]{1,0:T(8,128)} %copy.15.ids_ref, s32[64,1]{1,0:T(8,128)} %copy.16.dest_ref, s32[1,128]{1,0:T(1,128)} %bitcast.16, s32[1,128]{1,0:T(1,128)} %bitcast.17, f32[1,1]{1,0:T(1,128)} %bitcast.11.comp_ref, ...), custom_call_target="tpu_custom_call" | custom-call | tf_op jit(solution)/shard_map/fused_step/pallas_call | solution.py:550
  113.2 1.1 slice_bitcast_fusion
  114.3 1.7 %copy.21 = f32[1,64,1024]{2,1,0:T(8,128)} copy(f32[1,64,1024]{2,1,0:T(8,128)} %get-tuple-element.16) | data formatting | bytes 524288
  115.9 1.7 %copy.22 = f32[1,64,1024]{2,1,0:T(8,128)} copy(f32[1,64,1024]{2,1,0:T(8,128)} %get-tuple-element.17) | data formatting | bytes 524288
  (1 shorter events, 0.0 us)
Async XLA Ops:
  0.6 4.2 %copy-start = (bf16[128,8,1024]{2,1,0:T(8,128)(2,1)S(1)}, bf16[128,8,1024]{2,1,0:T(8,128)(2,1)}, u32[]{:S(2)}) copy-start(bf16[128,8,1024]{2,1,0:T(8,128)(2,1)} %param.12) | copy-start | bytes 6291460

commit v2 on v1

--- a/solution.py
+++ b/solution.py
@@ -142,11 +142,11 @@
 
 
 def fused_kernel(
-    ids_ref, dest_ref, bucket_ref, length_ref, comp_ref, gain_ref, x_ref, t_ref, frozen_ref, down_ref, up_ref,
+    ids_ref, dest_ref, bucket_ref, length_ref, comp_ref, gain_ref, x_ref, pool_ref, frozen_ref, down_ref, up_ref,
     gd_ref, gu_ref, loss_ref, next_ref,
-    frozen_buf, x_full, n_full, gain_full, adapters, counts_buf, loss_mp, loss_dp,
+    frozen_buf, pool_buf, t_ref, x_full, n_full, gain_full, adapters, counts_buf, loss_mp, loss_dp,
     m_dest, m_coef, m_live, m_bucket, gap, spread, grad_out, lat_own, lat_pair, lat_send, lat_recv,
-    grads, x_out, x_in, z_out, z_up, z_down,
+    grads, x_out, x_in, z_out, z_up, z_down, w_out, w_up, w_down,
     local_sem, xs_sem, xr_sem, gain_s, gain_r, au_s, au_r, ad_s, ad_r, ax_s, ax_r, cnt_s, cnt_r,
     lm_s, lm_r, ld_s, ld_r, l1_s, l1_r, l2_s, l2_r, gx_s, gx_r, gu_s, gu_r, gdn_s, gdn_r,
 ):
@@ -156,7 +156,7 @@
     z, xx = d // 2, d % 2
     tokens, part = x_ref.shape
     rank = down_ref.shape[1]
-    blocks = ids_ref.shape[0]
+    blocks = ids_ref.shape[1]
     block_len = tokens // blocks
     groups = n_dp * rank // LANES
     per_group = LANES // rank
@@ -213,8 +213,6 @@
         view = x_full.at[slot, rows]
         remote(view, view, xs_sem.at[kind, i], xr_sem.at[kind, i], (d, partner)).wait_recv()
 
-    for i in range(CHUNKS):
-        send(functools.partial(x_copy, 0, i))
     own_down.wait()
     own_up.wait()
 
@@ -231,6 +229,7 @@
     send(lambda: a_copy(2, z, x_peer))
     send(lambda: a_copy(0, z, d + 2), z < levels - 1)
     send(lambda: a_copy(1, z, d - 2), z > 0)
+    send(functools.partial(x_copy, 0, 0))
     for i in range(CHUNKS):
         send(functools.partial(x_copy, 1, i))
     gain_full[m] = gain_ref[...]
@@ -240,17 +239,19 @@
                 gain_ref, gain_full.at[m], gain_s.at[j], gain_r.at[j], (d, (m + j) % n_mp)
             )
         )
+    own_pool = pltpu.make_async_copy(pool_ref, pool_buf, local_sem.at[4])
+    own_pool.start()
     own_frozen.start()
 
     lane = lax.broadcasted_iota(jnp.int32, (tokens, LANES), 1)
     row = lax.broadcasted_iota(jnp.int32, (tokens, LANES), 0)
-    lane64 = lax.broadcasted_iota(jnp.int32, (blocks, LANES), 1)
-    named = jnp.where(lane64 < LANES // 2, ids_ref[...], dest_ref[...]).astype(f32).astype(bf16)
+    first_row = lax.broadcasted_iota(jnp.int32, (LANES, blocks), 0) < LANES // 2
+    named = jnp.where(first_row, ids_ref[...], dest_ref[...]).astype(f32).astype(bf16)
     spread_rows = (
         lax.broadcasted_iota(jnp.int32, (tokens, blocks), 0) // block_len
         == lax.broadcasted_iota(jnp.int32, (tokens, blocks), 1)
     ).astype(f32).astype(bf16)
-    per_token = jnp.dot(spread_rows, named, preferred_element_type=f32)
+    per_token = lax.dot_general(spread_rows, named, CONTRACT_LAST, preferred_element_type=f32)
     token_id, token_dest = per_token[:, 0:1], per_token[:, LANES // 2:LANES // 2 + 1]
     chosen = token_id == lane.astype(f32)
     token_bucket = jnp.sum(jnp.where(chosen, bucket_ref[...].astype(f32), 0.0), axis=1, keepdims=True)
@@ -258,6 +259,7 @@
     live = ((row % block_len).astype(f32) < token_length).astype(f32)
     bucket_hot = (token_bucket == lane.astype(f32)).astype(f32)
     m_dest[...] = jnp.broadcast_to(token_dest, (tokens, LANES))
+    m_coef[...] = jnp.broadcast_to(token_id, (tokens, LANES))
     m_live[...] = live
     m_bucket[...] = bucket_hot
     counts_buf[d] = jnp.broadcast_to(jnp.sum(bucket_hot * live, axis=0, keepdims=True), (8, LANES))
@@ -281,6 +283,20 @@
         source = (m + n_mp - j) % n_mp
         remote(gain_ref, gain_full.at[source], gain_s.at[j], gain_r.at[j], (d, source)).wait_recv()
     spread_tile(counts_buf, cnt_s, cnt_r, "dp")
+
+    own_pool.wait()
+
+    def pick_targets(i, carry):
+        rows = pl.ds(pl.multiple_of(i * 128, 128), 128)
+        stored = pool_buf.shape[0]
+        pool_row = lax.broadcasted_iota(jnp.int32, (128, stored), 1)
+        place = lax.broadcasted_iota(jnp.int32, (128, 1), 0) % block_len
+        wanted = m_coef[rows, 0:1] * block_len + place.astype(f32)
+        hot = (pool_row.astype(f32) == wanted).astype(f32).astype(bf16)
+        t_ref[rows, :] = jnp.dot(hot, pool_buf[...], preferred_element_type=f32).astype(bf16)
+        return carry
+
+    lax.fori_loop(0, tokens // 128, pick_targets, 0)
 
     def normalise(i):
         step = 32
@@ -330,19 +346,21 @@
         send(lambda: a_copy(2, z + s, x_peer), z + s < levels)
         send(lambda: a_copy(1, z + s, d - 2), (z + s < levels) & (z > 0))
 
+    for s in range(1, levels):
+        relay(s)
+        if s < CHUNKS:
+            send(functools.partial(x_copy, 0, s))
+    for i in range(levels, CHUNKS):
+        send(functools.partial(x_copy, 0, i))
     for i in range(CHUNKS):
         x_wait(0, i)
         send(functools.partial(x_copy, 2, i))
-        if 1 <= i < levels:
-            relay(i)
         x_wait(1, i)
         x_wait(2, i)
         normalise(i)
         if i == CHUNKS // 2 - 1:
             own_frozen.wait()
             project(0)
-    for s in range(CHUNKS, levels):
-        relay(s)
     for zt in range(levels):
         a_wait(2, zt, zt * 2 + (1 - xx))
 
@@ -447,7 +465,9 @@
             return carry
 
         lax.fori_loop(0, part // tile, body, 0)
-        for p in range(levels):
+
+    def send_sideways(h, positions):
+        for p in positions:
             if p == levels - 1:
                 zt = z
             else:
@@ -465,6 +485,7 @@
     gradient(1, lambda cols: grad_out[:, cols])
     second_half_sum(1)
     spread_tile(loss_mp, lm_s, lm_r, "mp")
+    send_sideways(1, range(2))
     finish_sum(1)
     gradient(0, lambda cols: n_full[m, :, cols])
 
@@ -479,42 +500,77 @@
         remote(view, view, s_sem.at[h, zt], r_sem.at[h, zt], (x_peer, m)).wait_recv()
         grads[h, zt * 2 + xx] += buf[h, zt].astype(f32)
 
-    def pass_on(h, s):
+    def came(buf, zt, s_sem, r_sem):
+        view = buf.at[zt]
+        remote(view, view, s_sem.at[0, zt], r_sem.at[0, zt], (x_peer, m)).wait_recv()
+        grads[0, pl.ds(zt * 2, 2)] += buf[zt].astype(f32)
+
+    def pass_pair(s):
         def upward():
             zt = z + s
-            arrived(x_in, h, zt, gx_s, gx_r)
-            pl.when(z > 0)(lambda: arrived(z_up, h, zt, gu_s, gu_r))
-            z_out[h, zt] = grads[h, zt * 2 + xx].astype(bf16)
+            pl.when(z > 0)(lambda: came(w_up, zt, gu_s, gu_r))
+            w_out[zt] = grads[0, pl.ds(zt * 2, 2)].astype(bf16)
 
         def downward():
             zt = z - s
-            arrived(x_in, h, zt, gx_s, gx_r)
-            pl.when(z < levels - 1)(lambda: arrived(z_down, h, zt, gdn_s, gdn_r))
-            z_out[h, zt] = grads[h, zt * 2 + xx].astype(bf16)
+            pl.when(z < levels - 1)(lambda: came(w_down, zt, gdn_s, gdn_r))
+            w_out[zt] = grads[0, pl.ds(zt * 2, 2)].astype(bf16)
+
+        pl.when(z + s < levels)(upward)
+        send(
+            lambda: remote(w_out.at[z + s], w_up.at[z + s], gu_s.at[0, z + s], gu_r.at[0, z + s], (d + 2, m)),
+            z + s < levels,
+        )
+        pl.when(z - s >= 0)(downward)
+        send(
+            lambda: remote(w_out.at[z - s], w_down.at[z - s], gdn_s.at[0, z - s], gdn_r.at[0, z - s], (d - 2, m)),
+            z - s >= 0,
+        )
+
+    def pass_on(s):
+        def upward():
+            zt = z + s
+            arrived(x_in, 1, zt, gx_s, gx_r)
+            pl.when(z > 0)(lambda: arrived(z_up, 1, zt, gu_s, gu_r))
+            z_out[1, zt] = grads[1, zt * 2 + xx].astype(bf16)
+
+        def downward():
+            zt = z - s
+            arrived(x_in, 1, zt, gx_s, gx_r)
+            pl.when(z < levels - 1)(lambda: arrived(z_down, 1, zt, gdn_s, gdn_r))
+            z_out[1, zt] = grads[1, zt * 2 + xx].astype(bf16)
 
         pl.when(z + s < levels)(upward)
         send(
             lambda: remote(
-                z_out.at[h, z + s], z_up.at[h, z + s], gu_s.at[h, z + s], gu_r.at[h, z + s], (d + 2, m)
+                z_out.at[1, z + s], z_up.at[1, z + s], gu_s.at[1, z + s], gu_r.at[1, z + s], (d + 2, m)
             ),
             z + s < levels,
         )
         pl.when(z - s >= 0)(downward)
         send(
             lambda: remote(
-                z_out.at[h, z - s], z_down.at[h, z - s], gdn_s.at[h, z - s], gdn_r.at[h, z - s], (d - 2, m)
+                z_out.at[1, z - s], z_down.at[1, z - s], gdn_s.at[1, z - s], gdn_r.at[1, z - s], (d - 2, m)
             ),
             z - s >= 0,
         )
 
     spread_tile(loss_dp, ld_s, ld_r, "dp")
-    for h, out_ref in ((1, gu_ref), (0, gd_ref)):
-        for s in range(levels - 1, 0, -1):
-            pass_on(h, s)
-        arrived(x_in, h, z, gx_s, gx_r)
-        pl.when(z > 0)(lambda h=h: arrived(z_up, h, z, gu_s, gu_r))
-        pl.when(z < levels - 1)(lambda h=h: arrived(z_down, h, z, gdn_s, gdn_r))
-        out_ref[0] = grads[h, d]
+    for s in range(levels - 1, 0, -1):
+        pass_pair(s)
+        if levels - s >= 2:
+            send_sideways(1, (levels - s,))
+        pass_on(s)
+    pl.when(z > 0)(lambda: came(w_up, z, gu_s, gu_r))
+    pl.when(z < levels - 1)(lambda: came(w_down, z, gdn_s, gdn_r))
+    x_out[0, z] = grads[0, z * 2 + (1 - xx)].astype(bf16)
+    send(lambda: remote(x_out.at[0, z], x_in.at[0, z], gx_s.at[0, z], gx_r.at[0, z], (x_peer, m)))
+    arrived(x_in, 1, z, gx_s, gx_r)
+    pl.when(z > 0)(lambda: arrived(z_up, 1, z, gu_s, gu_r))
+    pl.when(z < levels - 1)(lambda: arrived(z_down, 1, z, gdn_s, gdn_r))
+    gu_ref[0] = grads[1, d]
+    arrived(x_in, 0, z, gx_s, gx_r)
+    gd_ref[0] = grads[0, d]
 
     gather_tile(loss_dp, ld_s, ld_r, "dp")
     loss_sum = loss_dp[0]
@@ -542,8 +598,8 @@
     rank = adapter_down.shape[1]
     tokens = blocks * block_len
     levels = n_dp // 2
-    x = pool_inputs.at[sample_ids].get(mode="promise_in_bounds").reshape(tokens, part)
-    t = pool_targets.at[sample_ids].get(mode="promise_in_bounds").reshape(tokens, part)
+    x = pool_inputs.at[sample_ids].get(mode="promise_in_bounds", wrap_negative_indices=False).reshape(tokens, part)
+    t = pool_targets.reshape(pool * block_len, part)
     f32, bf16 = jnp.float32, jnp.bfloat16
     vmem = pl.BlockSpec(memory_space=pltpu.VMEM)
     dma = pltpu.SemaphoreType.DMA
@@ -555,10 +611,12 @@
             jax.ShapeDtypeStruct((1, LANES), f32),
             jax.ShapeDtypeStruct((1, LANES), f32),
         ),
-        in_specs=[vmem] * 8 + [pl.BlockSpec(memory_space=pl.ANY)] + [vmem] * 2,
+        in_specs=[vmem] * 7 + [pl.BlockSpec(memory_space=pl.ANY)] * 2 + [vmem] * 2,
         out_specs=(vmem,) * 4,
         scratch_shapes=[
             pltpu.VMEM(frozen.shape, bf16),
+            pltpu.VMEM(t.shape, bf16),
+            pltpu.VMEM((tokens, part), bf16),
             pltpu.VMEM((n_mp, tokens, part), bf16),
             pltpu.VMEM((n_mp, tokens, part), bf16),
             pltpu.VMEM((n_mp, 1, part), f32),
@@ -583,7 +641,10 @@
             pltpu.VMEM((2, levels, rank, part), bf16),
             pltpu.VMEM((2, levels, rank, part), bf16),
             pltpu.VMEM((2, levels, rank, part), bf16),
-            dma((4,)), dma((3, CHUNKS)), dma((3, CHUNKS)), dma((n_mp,)), dma((n_mp,)),
+            pltpu.VMEM((levels, 2, rank, part), bf16),
+            pltpu.VMEM((levels, 2, rank, part), bf16),
+            pltpu.VMEM((levels, 2, rank, part), bf16),
+            dma((5,)), dma((3, CHUNKS)), dma((3, CHUNKS)), dma((n_mp,)), dma((n_mp,)),
             dma((levels,)), dma((levels,)), dma((levels,)), dma((levels,)), dma((levels,)), dma((levels,)),
             dma((n_dp,)), dma((n_dp,)), dma((n_mp,)), dma((n_mp,)), dma((n_dp,)), dma((n_dp,)),
             dma((2,)), dma((2,)), dma((2,)), dma((2,)),
@@ -594,7 +655,7 @@
         ),
         name="fused_step",
     )(
-        sample_ids[:, None], destinations, buckets[None, :], lengths[None, :], competence[:, None], gain[None, :],
+        sample_ids[None, :], destinations.reshape(1, blocks), buckets[None, :], lengths[None, :], competence[:, None], gain[None, :],
         x, t, frozen, adapter_down, adapter_up,
     )
     return out[0], out[1], out[2][0, :NB], out[3][0, :1]
@@ -605,7 +666,7 @@
         pool_inputs, frozen, adapter_down, sample_ids = args[0], args[2], args[4], args[6]
         tokens, part = sample_ids.shape[0] * pool_inputs.shape[1], pool_inputs.shape[2]
         n_dp, n_mp, rank = lax.axis_size("dp"), lax.axis_size("mp"), adapter_down.shape[1]
-        held = 2 * frozen.size + 4 * n_mp * tokens * part + (26 * n_dp + 16) * rank * part
+        held = 2 * frozen.size + 4 * n_mp * tokens * part + (32 * n_dp + 16) * rank * part + 2 * pool_inputs.size
         fits = held < 44 * 2**20 and n_mp == 4 and n_dp % 2 == 0 and n_dp > 2
         exact = pool_inputs.shape[0] == LANES and n_dp * rank % LANES == 0 and LANES % rank == 0
         return (on_device_fused if fits and exact else on_device)(*args)

time: 120 us -> 101 us (0.84)
  Pallas kernels: 104 us -> 90.4 us
  local copies, waits for them, and re-layouts: 12 us -> 6.21 us
    pallas_call x1, Pallas kernels: 104 us -> 90.4 us  [on_device_fused(): pl.pallas_call(fused_kernel, out_shape=(jax.ShapeDtypeStruct((1, rank, pa...]
    gather x2 -> x1, local copies, waits for them, and re-layouts: 4.81 us -> 1.59 us  [on_device_fused(): pool_inputs.at[sample_ids]]
    broadcast_in_dim x1 -> x0, local copies, waits for them, and re-layouts: 1.36 us -> none  [on_device_fused(): sample_ids[:, None]]
    unnamed x5 -> x4, local copies, waits for them, and re-layouts: 4.71 us -> 3.49 us
where the time goes in v2:
time: 101 us; the launch traced here: 100 us
  Pallas kernels  90.4 us (90%)
  local copies, waits for them, and re-layouts  6.21 us (6%)
  between operations  3.21 us (3%)
    pallas_call x1, Pallas kernels, on_device_fused(): pl.pallas_call(fused_kernel, out_shape=(jax.ShapeDtypeStruct((1, rank, pa...  90.4 us
    unnamed x4, local copies, waits for them, and re-layouts  3.49 us

profile of v2, /device:TPU:0, one launch (start us, length us, event | category | flops | bytes accessed | tf_op | source)
XLA Modules:
  0.0 100.5 jit_solution(14006682812392191251)
XLA Ops:
  0.6 0.0 copy-start
  1.4 0.7 pad_clamp_fusion
  2.1 0.1 copy-done
  2.2 1.6 %gather_fusion = bf16[64,8,1024]{2,1,0:T(8,128)(2,1)} fusion(bf16[128,8,1024]{2,1,0:T(8,128)(2,1)S(1)} %copy-done, s32[1024]{0:T(1024)S(1)} %pad_clamp_fusion), kind=kCustom, calls=%fused_computation | custom fusion | bytes 2097408 | tf_op jit(solution)/shard_map/gather | solution.py:601
  3.8 90.4 %fused_step.1 = (f32[1,64,1024]{2,1,0:T(8,128)}, f32[1,64,1024]{2,1,0:T(8,128)}, f32[1,128]{1,0:T(1,128)}, f32[1,128]{1,0:T(1,128)}) custom-call(s32[1,64]{1,0:T(1,128)} %bitcast.16, s32[1,64]{1,0:T(1,128)} %bitcast.17, s32[1,128]{1,0:T(1,128)} %bitcast.18, s32[1,128]{1,0:T(1,128)} %bitcast.19, f32[1,1]{1,0:T(1,128)} %bitcast.12.comp_ref, ...), custom_call_target="tpu_custom_call" | custom-call | tf_op jit(solution)/shard_map/fused_step/pallas_call | solution.py:606
  94.2 1.1 %slice_bitcast_fusion = f32[16]{0:T(128)} fusion(f32[1,128]{1,0:T(1,128)} %get-tuple-element.10), kind=kLoop, calls=%fused_computation.2 | loop fusion | bytes 128 | tf_op jit(solution)/shard_map/squeeze | solution.py:661
  95.4 1.7 %copy.19 = f32[1,64,1024]{2,1,0:T(8,128)} copy(f32[1,64,1024]{2,1,0:T(8,128)} %get-tuple-element.16) | data formatting | bytes 524288
  97.0 1.7 %copy.20 = f32[1,64,1024]{2,1,0:T(8,128)} copy(f32[1,64,1024]{2,1,0:T(8,128)} %get-tuple-element.17) | data formatting | bytes 524288
Async XLA Ops:
  0.6 1.6 %copy-start = (bf16[128,8,1024]{2,1,0:T(8,128)(2,1)S(1)}, bf16[128,8,1024]{2,1,0:T(8,128)(2,1)}, u32[]{:S(2)}) copy-start(bf16[128,8,1024]{2,1,0:T(8,128)(2,1)} %param.11) | copy-start | bytes 6291460
